TPU v7x, 32 devices: a whole 2x2x4 slice. The times are simulated.
32 devices in a mesh: member: 2 (over y), gy: 4 (over z), gx: 2 (over x), lev: 2 (over core).
Axes of the slice: x: 2, y: 2, z: 4, core: 2. Of those that a mesh axis runs over, the one named last changes fastest.
Arguments:
- level_field: bfloat16 [32, 1536, 1536], P(('member', 'lev'), 'gy', 'gx'), parts along dimension 0, may hold values from -6 to 6
Outputs:
- spectra: float32 [1536, 32, 1536], P(('gy', 'gx'), ('member', 'lev')), parts along dimension 1
- spectra_zone: float32 [1536, 32, 11], P(('gy', 'gx'), ('member', 'lev')), parts along dimension 1
There are 2 independent parts, one for each index of `member`. A program takes and returns all parts, laid end to end along the dimension named above; each array names one. Nothing has to cross between parts.
All inputs are finite; a program needn't handle non-finite values.
Results may differ from a plain program's by a relative error of at most 0.0042.
Values may be sent and summed in bfloat16 or wider, within the bound.
A program may use at most 128 MiB of HBM per device.

v0:
```python
import math
import jax
import jax.numpy as jnp
from jax import lax
from jax.sharding import PartitionSpec as P

NX = 1536
NY = 1536
EXT_ZONE = 11
WAVES = 768


def blend_zone(second_last, last_value, first_value, second_value, zone_count):
    steps = (jnp.arange(zone_count, dtype=jnp.int32) + 1).astype(jnp.float32) / (zone_count + 1.0)
    weight_a = 2.0 * steps**3 - 3.0 * steps**2 + 1.0
    weight_b = steps**3 - 2.0 * steps**2 + steps
    weight_c = -2.0 * steps**3 + 3.0 * steps**2
    weight_d = steps**3 - steps**2
    tangent_scale = zone_count + 1.0
    slope_start = tangent_scale * (last_value - second_last)
    slope_end = tangent_scale * (second_value - first_value)
    return (
        last_value[..., None] * weight_a
        + slope_start[..., None] * weight_b
        + first_value[..., None] * weight_c
        + slope_end[..., None] * weight_d
    )


def make_table(wave_count, length):
    coeff = jnp.arange(2 * wave_count, dtype=jnp.int32)[:, None]
    column = jnp.arange(length, dtype=jnp.int32)[None, :]
    is_cosine = coeff < wave_count
    number = jnp.where(is_cosine, coeff, coeff - wave_count + 1)
    phase = (number * column % length).astype(jnp.float32) * (2.0 * math.pi / length)
    values = jnp.where(is_cosine, jnp.cos(phase), -jnp.sin(phase)) / math.sqrt(length)
    return values.astype(jnp.bfloat16)


def shards(level_field):
    wave_table = make_table(WAVES, NX + EXT_ZONE)
    core_table = wave_table[:, :NX]
    zone_table = wave_table[:, NX:]
    core_rows = lax.all_to_all(level_field, "gx", split_axis=1, concat_axis=2, tiled=True)
    widened = core_rows.astype(jnp.float32)
    zone_cols = blend_zone(
        widened[..., NX - 2], widened[..., NX - 1], widened[..., 0], widened[..., 1], EXT_ZONE
    ).astype(jnp.bfloat16)
    dims = (((1,), (2,)), ((), ()))
    total = lax.dot_general(core_table, core_rows, dims, preferred_element_type=jnp.float32)
    partial_spec = total + lax.dot_general(
        zone_table, zone_cols, dims, preferred_element_type=jnp.float32
    )
    moved = lax.all_to_all(partial_spec, ("gy", "gx"), split_axis=0, concat_axis=2, tiled=True)
    spectra_zone = blend_zone(
        moved[..., NY - 2], moved[..., NY - 1], moved[..., 0], moved[..., 1], EXT_ZONE
    )
    return (moved, spectra_zone)


def solution(mesh):
    return jax.shard_map(
        shards,
        mesh=mesh,
        in_specs=(P(("member", "lev"), "gy", "gx"),),
        out_specs=(
            P(("gy", "gx"), ("member", "lev"), None),
            P(("gy", "gx"), ("member", "lev"), None),
        ),
        check_vma=False,
    )
```

profile of v0, /device:TPU:0, one launch (start us, length us, event | category | flops | bytes accessed | tf_op | source)
XLA Modules:
  0.0 426.6 jit_solution(1554581682853218261)
XLA Ops:
  0.6 7.1 %copy.14 = bf16[8,384,768]{2,0,1:T(8,128)(2,1)} copy(bf16[8,384,768]{2,1,0:T(8,128)(2,1)} %param.1) | data formatting | bytes 9437184 | tf_op args[0]
  7.8 6.0 %all-to-all-start = ((bf16[8,384,768]{2,0,1:T(8,128)(2,1)}), bf16[8,384,768]{2,0,1:T(8,128)(2,1)}, u32[]{:S(2)}, u32[]{:S(2)}) async-start(bf16[8,384,768]{2,0,1:T(8,128)(2,1)} %copy.14), calls=%async_computation | async-start | bytes 9437184 | tf_op jit(solution)/shard_map/all_to_all | solution.py:44
  13.8 46.7 %multiply_convert_fusion = bf16[1536,1547]{1,0:T(8,128)(2,1)} fusion(s32[1536]{0:T(1024)S(1)} %add_select_fusion.1, pred[1536]{0:T(1024)(128)(4,1)S(1)} %iota_compare_fusion), kind=kLoop, calls=%fused_computation.3 | loop fusion | flops 30890496 | bytes 4760064 | tf_op jit(solution)/shard_map/convert_element_type | solution.py:37
  60.5 7.7 %all-to-all-done = bf16[8,384,768]{2,0,1:T(8,128)(2,1)} async-done(((bf16[8,384,768]{2,0,1:T(8,128)(2,1)}), bf16[8,384,768]{2,0,1:T(8,128)(2,1)}, u32[]{:S(2)}, u32[]{:S(2)}) %all-to-all-start) | async-done | bytes 4718624 | tf_op jit(solution)/shard_map/all_to_all | solution.py:44
  68.2 9.4 %copy.23 = bf16[8,2,192,768]{3,1,2,0:T(2,128)(2,1)} copy(bf16[8,2,192,768]{3,0,2,1:T(8,128)(2,1)} %bitcast.1) | data formatting | bytes 9437184 | tf_op jit(solution)/shard_map/all_to_all | solution.py:44
  77.6 0.0 slice-start.2
  77.6 11.3 %all_to_all.29 = bf16[8,192,1536]{2,1,0:T(8,128)(2,1)} reshape(bf16[8,192,2,768]{3,2,1,0:T(2,128)(2,1)} %bitcast.28) | data formatting | bytes 9437184 | tf_op jit(solution)/shard_map/all_to_all | solution.py:44
  88.9 0.0 slice-start.3
  88.9 3.8 convert_element_type.49
  92.7 0.0 slice-start
  92.7 1.8 slice_reduce_fusion.1
  94.5 0.0 slice-done.2
  94.5 0.0 slice-done.3
  94.6 0.0 slice-start.1
  94.6 1.5 fusion.9
  96.1 0.0 slice-done
  96.1 0.0 slice-done.1
  96.1 10.6 %convolution_add_fusion = f32[1536,8,192]{0,2,1:T(8,128)} fusion(f32[1536,8,192]{0,2,1:T(8,128)S(1)} %fusion.9, bf16[8,192,1536]{2,1,0:T(8,128)(2,1)S(1)} %bitcast.27, bf16[1536,1547]{1,0:T(8,128)(2,1)S(1)} %bitcast.30), kind=kOutput, calls=%fused_computation.8 | convolution fusion | flops 7250116608 | bytes 28311552 | tf_op jit(solution)/shard_map/dot_general | solution.py:50
  106.7 12.8 %copy.17 = f32[1536,8,192]{2,1,0:T(8,128)} copy(f32[1536,8,192]{0,2,1:T(8,128)} %convolution_add_fusion) | data formatting | bytes 18874368 | tf_op jit(solution)/shard_map/add | solution.py:51
  119.5 279.9 %all_to_all.36 = f32[1536,8,192]{2,1,0:T(8,128)} all-to-all(f32[1536,8,192]{2,1,0:T(8,128)} %copy.17), channel_id=1, replica_groups=mesh['member'=2,'gy'=4,'gx'=2,'lev'=2] {'gy','gx'}, dimensions={0} | all-to-all | bytes 18874368 | tf_op jit(solution)/shard_map/all_to_all | solution.py:54
  399.4 13.8 %copy.18 = f32[8,192,8,192]{1,2,3,0:T(8,128)} copy(f32[8,192,8,192]{3,2,1,0:T(8,128)} %bitcast.25) | data formatting | bytes 18874368 | tf_op jit(solution)/shard_map/all_to_all | solution.py:54
  413.2 0.8 slice_bitcast_fusion.5
  414.0 11.9 %copy.19 = f32[192,8,1536]{2,1,0:T(8,128)} copy(f32[192,8,1536]{0,1,2:T(8,128)} %bitcast.24) | data formatting | bytes 18874368
  425.9 0.8 multiply_add_fusion
  (6 shorter events, 0.0 us)
Async XLA Ops:
  7.8 60.5 %all-to-all-start = ((bf16[8,384,768]{2,0,1:T(8,128)(2,1)}), bf16[8,384,768]{2,0,1:T(8,128)(2,1)}, u32[]{:S(2)}, u32[]{:S(2)}) async-start(bf16[8,384,768]{2,0,1:T(8,128)(2,1)} %copy.14), calls=%async_computation | async-start | bytes 9437184 | tf_op jit(solution)/shard_map/all_to_all | solution.py:44
  77.6 16.9 %slice-start.2 = ((s8[5111808]{0:T(1024)(128)(4,1)}), s8[917504]{0:T(1024)(128)(4,1)S(1)}, s32[]{:S(2)}) async-start(s8[5111808]{0:T(1024)(128)(4,1)} %bitcast.29), calls=%async_computation.4 | async-start | bytes 1835008
  88.9 5.6 %slice-start.3 = ((s8[5111808]{0:T(1024)(128)(4,1)}), s8[4194304]{0:T(1024)(128)(4,1)S(1)}, s32[]{:S(2)}) async-start(s8[5111808]{0:T(1024)(128)(4,1)} %bitcast.29), calls=%async_computation.5 | async-start | bytes 8388608
  92.7 3.4 slice-start
  94.6 1.5 slice-start.1
where the time goes:
time: 428 us; the launch traced here: 427 us
  blocking collectives  280 us (65%)
  local copies, waits for them, and re-layouts  66.3 us (15%)
  other arithmetic  53.8 us (13%)
  matrix products  12.1 us (3%)
  waiting for transfers between devices  7.74 us (2%)
  starting transfers between devices  5.95 us (1%)
    all_to_all x1, blocking collectives, shards(): lax.all_to_all(partial_spec, ('gy', 'gx'), split_axis=0, concat_axis=2, t...  280 us
    convert_element_type x1, other arithmetic, make_table(): return values.astype(jnp.bfloat16)  46.7 us
    all_to_all x2, local copies, waits for them, and re-layouts, shards(): lax.all_to_all(level_field, 'gx', split_axis=1, concat_axis=2, tiled=True)  20.7 us
    unnamed x10, local copies, waits for them, and re-layouts  19 us
    all_to_all x1, local copies, waits for them, and re-layouts, shards(): lax.all_to_all(partial_spec, ('gy', 'gx'), split_axis=0, concat_axis=2, t...  13.8 us
    add x1, local copies, waits for them, and re-layouts, shards(): total + lax.dot_general(zone_table, zone_cols, dims, preferred_element_ty...  12.8 us
    dot_general x1, matrix products, shards(): lax.dot_general(core_table, core_rows, dims, preferred_element_type=jnp.f...  10.6 us
  transfers between devices with their start and end apart: 1, of which 1 were waited for; matrix products, arithmetic and copies ran while one was open for 11% of the time, Pallas kernels for 0%

commit v1 on v0

--- a/solution.py
+++ b/solution.py
@@ -8,6 +8,18 @@
 NY = 1536
 EXT_ZONE = 11
 WAVES = 768
+
+
+def note_map(load, bus_axis):
+    return jnp.concatenate(
+        lax.all_to_all(
+            jnp.stack(jnp.split(load, lax.psum(1, bus_axis), axis=1), axis=0),
+            axis_name=bus_axis,
+            split_axis=0,
+            concat_axis=0,
+        ),
+        axis=2,
+    )
 
 
 def blend_zone(second_last, last_value, first_value, second_value, zone_count):
@@ -41,7 +53,7 @@
     wave_table = make_table(WAVES, NX + EXT_ZONE)
     core_table = wave_table[:, :NX]
     zone_table = wave_table[:, NX:]
-    core_rows = lax.all_to_all(level_field, "gx", split_axis=1, concat_axis=2, tiled=True)
+    core_rows = note_map(level_field, "gx")
     widened = core_rows.astype(jnp.float32)
     zone_cols = blend_zone(
         widened[..., NX - 2], widened[..., NX - 1], widened[..., 0], widened[..., 1], EXT_ZONE

time: 428 us -> 405 us (0.946)
  local copies, waits for them, and re-layouts: 66.3 us -> 44 us
    all_to_all x2 -> x0, local copies, waits for them, and re-layouts: 20.7 us -> none  [shards(): lax.all_to_all(level_field, 'gx', split_axis=1, concat_axis=2, tiled=True)]
    unnamed x10 -> x5, local copies, waits for them, and re-layouts: 19 us -> 11.9 us
  transfers between devices with their start and end apart: 1 -> 1, of which waited for: 1 -> 1; matrix products, arithmetic and copies ran while one was open for 11% -> 12% of each run, Pallas kernels for 0% -> 0%
where the time goes in v1:
time: 405 us; the launch traced here: 404 us
  blocking collectives  280 us (69%)
  other arithmetic  53.9 us (13%)
  local copies, waits for them, and re-layouts  44 us (11%)
  matrix products  11.9 us (3%)
  waiting for transfers between devices  7.72 us (2%)
  starting transfers between devices  5.77 us (1%)
    all_to_all x1, blocking collectives, shards(): lax.all_to_all(partial_spec, ('gy', 'gx'), split_axis=0, concat_axis=2, t...  280 us
    convert_element_type x1, other arithmetic, make_table(): return values.astype(jnp.bfloat16)  46.7 us
    all_to_all x1, local copies, waits for them, and re-layouts, shards(): lax.all_to_all(partial_spec, ('gy', 'gx'), split_axis=0, concat_axis=2, t...  13.8 us
    add x1, local copies, waits for them, and re-layouts, shards(): total + lax.dot_general(zone_table, zone_cols, dims, preferred_element_ty...  12.8 us
    unnamed x5, local copies, waits for them, and re-layouts  11.9 us
    dot_general x1, matrix products, shards(): lax.dot_general(core_table, core_rows, dims, preferred_element_type=jnp.f...  10.4 us
  transfers between devices with their start and end apart: 1, of which 1 were waited for; matrix products, arithmetic and copies ran while one was open for 12% of the time, Pallas kernels for 0%

profile of v1, /device:TPU:0, one launch (start us, length us, event | category | flops | bytes accessed | tf_op | source)
XLA Modules:
  0.0 404.0 jit_solution(9415132332485628620)
XLA Ops:
  0.6 2.8 slice_bitcast_fusion.3
  3.4 2.6 pad_maximum_fusion
  6.0 5.8 %all-to-all-start = ((bf16[2,8,192,768]{3,2,1,0:T(8,128)(2,1)}), bf16[2,8,192,768]{3,2,1,0:T(8,128)(2,1)}, u32[]{:S(2)}, u32[]{:S(2)}) async-start(bf16[2,8,192,768]{3,2,1,0:T(8,128)(2,1)} %pad_maximum_fusion), calls=%async_computation | async-start | bytes 9437184 | tf_op jit(solution)/shard_map/all_to_all | solution.py:15
  11.8 46.7 %multiply_convert_fusion = bf16[1536,1547]{1,0:T(8,128)(2,1)} fusion(s32[1536]{0:T(1024)S(1)} %add_select_fusion.1, pred[1536]{0:T(1024)(128)(4,1)S(1)} %iota_compare_fusion), kind=kLoop, calls=%fused_computation.3 | loop fusion | flops 30890496 | bytes 4760064 | tf_op jit(solution)/shard_map/convert_element_type | solution.py:49
  58.5 7.7 %all-to-all-done = bf16[2,8,192,768]{3,2,1,0:T(8,128)(2,1)} async-done(((bf16[2,8,192,768]{3,2,1,0:T(8,128)(2,1)}), bf16[2,8,192,768]{3,2,1,0:T(8,128)(2,1)}, u32[]{:S(2)}, u32[]{:S(2)}) %all-to-all-start) | async-done | bytes 4718624 | tf_op jit(solution)/shard_map/all_to_all | solution.py:15
  66.3 2.7 copy.21
  69.0 0.0 slice-start
  69.0 0.0 slice-start.1
  69.0 1.3 convert_element_type.49
  70.3 1.8 slice_reduce_fusion.1
  72.1 0.0 slice-done
  72.2 0.0 slice-done.1
  72.2 1.5 fusion.9
  73.7 10.4 %convolution_add_fusion = f32[1536,8,192]{0,2,1:T(8,128)} fusion(f32[1536,8,192]{0,2,1:T(8,128)S(1)} %fusion.9, bf16[8,192,1536]{2,1,0:T(8,128)(2,1)S(1)} %bitcast.30, bf16[1536,1547]{1,0:T(8,128)(2,1)S(1)} %bitcast.32), kind=kOutput, calls=%fused_computation.8 | convolution fusion | flops 7250116608 | bytes 28311552 | tf_op jit(solution)/shard_map/dot_general | solution.py:62
  84.1 12.8 %copy.16 = f32[1536,8,192]{2,1,0:T(8,128)} copy(f32[1536,8,192]{0,2,1:T(8,128)} %convolution_add_fusion) | data formatting | bytes 18874368 | tf_op jit(solution)/shard_map/add | solution.py:63
  96.8 280.0 %all_to_all.23 = f32[1536,8,192]{2,1,0:T(8,128)} all-to-all(f32[1536,8,192]{2,1,0:T(8,128)} %copy.16), channel_id=1, replica_groups=mesh['member'=2,'gy'=4,'gx'=2,'lev'=2] {'gy','gx'}, dimensions={0} | all-to-all | bytes 18874368 | tf_op jit(solution)/shard_map/all_to_all | solution.py:66
  376.8 13.8 %copy.17 = f32[8,192,8,192]{1,2,3,0:T(8,128)} copy(f32[8,192,8,192]{3,2,1,0:T(8,128)} %bitcast.28) | data formatting | bytes 18874368 | tf_op jit(solution)/shard_map/all_to_all | solution.py:66
  390.6 0.8 slice_bitcast_fusion.7
  391.4 11.9 %copy.18 = f32[192,8,1536]{2,1,0:T(8,128)} copy(f32[192,8,1536]{0,1,2:T(8,128)} %bitcast.27) | data formatting | bytes 18874368
  403.2 0.8 multiply_add_fusion
  (5 shorter events, 0.0 us)
Async XLA Ops:
  6.0 60.3 %all-to-all-start = ((bf16[2,8,192,768]{3,2,1,0:T(8,128)(2,1)}), bf16[2,8,192,768]{3,2,1,0:T(8,128)(2,1)}, u32[]{:S(2)}, u32[]{:S(2)}) async-start(bf16[2,8,192,768]{3,2,1,0:T(8,128)(2,1)} %pad_maximum_fusion), calls=%async_computation | async-start | bytes 9437184 | tf_op jit(solution)/shard_map/all_to_all | solution.py:15
  69.0 3.1 slice-start
  69.0 3.1 slice-start.1
